TPU v7x, 32 devices: a whole 2x2x4 slice. The times are simulated.
32 devices in a mesh: blk: 8 (over z, x), tgt: 4 (over y, core).
Axes of the slice: x: 2, y: 2, z: 4, core: 2. Of those that a mesh axis runs over, the one named last changes fastest.
Arguments:
- sources: float32 [8192, 128], P('blk'), may hold values from -0.5 to 0.5, as said below
- targets: float32 [8192, 128], P(('blk', 'tgt')), may hold values from -0.5 to 0.5, as said below
- duals_init: float32 [8192], P(('blk', 'tgt')), may hold values from -1.5 to 1.5
Outputs:
- source_duals: float32 [8192], P('blk')
- target_duals: float32 [8192], P(('blk', 'tgt'))
Inputs may be any that keep to these rules, and one draw needn't show every extreme that they name: `sources`: coordinates of the source points. `targets`: coordinates of the target points.
All inputs are finite; a program needn't handle non-finite values.
Results may differ from a plain program's by a relative error of at most 0.0001.
Values sent between devices are 32-bit elements; how exact they have to be, the bound alone decides.
A program may use at most 64 MiB of HBM per device.

v0:
```python
import jax
import jax.numpy as jnp
from jax import lax
from jax.sharding import PartitionSpec as P

ITERS = 2
EPS = 0.05


def cost_of(left, left_norm, right, right_norm):
    cross = jnp.dot(
        left, right.T, preferred_element_type=jnp.float32, precision=lax.Precision.HIGHEST
    )
    return left_norm[:, None] + right_norm[None, :] - 2.0 * cross


def body(sources, targets, duals_init):
    src_norm = jnp.sum(sources * sources, axis=1)
    rows_here = sources.shape[0]
    cols_here = targets.shape[0]
    total_dst = cols_here * lax.axis_size("blk") * lax.axis_size("tgt")
    total_src = rows_here * lax.axis_size("blk")
    target_pots = duals_init
    source_pots = jnp.zeros_like(src_norm)
    group_rows = lax.all_gather(targets, "blk", axis=0, tiled=True)
    group_norm = jnp.sum(group_rows * group_rows, axis=1)
    cost_tile = cost_of(sources, src_norm, group_rows, group_norm)
    for repeat in range(ITERS):
        group_pots = lax.all_gather(target_pots, "blk", axis=0, tiled=True)
        scores = (group_pots[None, :] - cost_tile) / EPS
        maxima = jnp.max(scores, axis=1)
        totals = jnp.sum(jnp.exp(scores - maxima[:, None]), axis=1)
        highest = lax.pmax(maxima, "tgt")
        totals = lax.psum(totals * jnp.exp(maxima - highest), "tgt")
        maxima = highest
        source_pots = EPS * -jnp.log(jnp.float32(total_dst)) - EPS * (maxima + jnp.log(totals))
        col_scores = (source_pots[:, None] - cost_tile) / EPS
        col_high = lax.pmax(jnp.max(col_scores, axis=0), "blk")
        col_part = jnp.sum(jnp.exp(col_scores - col_high[None, :]), axis=0)
        col_total = lax.psum_scatter(col_part, "blk", scatter_dimension=0, tiled=True)
        own_high = lax.dynamic_slice_in_dim(
            col_high, lax.axis_index("blk") * cols_here, cols_here, 0
        )
        target_pots = EPS * -jnp.log(jnp.float32(total_src)) - EPS * (own_high + jnp.log(col_total))
    return (source_pots, target_pots)


def solution(mesh):
    return jax.shard_map(
        body,
        mesh=mesh,
        in_specs=(P("blk", None), P(("blk", "tgt"), None), P(("blk", "tgt"))),
        out_specs=(P("blk"), P(("blk", "tgt"))),
        check_vma=False,
    )
```

profile of v0, /device:TPU:0, one launch (start us, length us, event | category | flops | bytes accessed | tf_op | source)
XLA Modules:
  0.0 220.8 jit_solution(6186228106651673261)
XLA Ops:
  7.2 0.0 all-gather.4.cloned.1.call-start
  7.2 0.7 all-gather.4.cloned.1.call-update
  7.9 1.2 dynamic-slice
  9.8 22.5 %all-gather = f32[8,1,256]{2,1,0:T(1,128)S(1)} all-gather(f32[1,1,256]{2,1,0:T(1,128)} %bitcast.12), channel_id=1, replica_groups=mesh['blk'=8,'tgt'=4] {'blk'}, dimensions={0}, use_global_device_ids=true | all-gather | bytes 9216 | tf_op jit(solution)/shard_map/all_gather | solution.py:29
  32.3 1.2 multiply_reduce_fusion.1
  33.6 19.5 %all-gather.4.cloned.1.call-done = f32[2048,128]{1,0:T(8,128)} async-done(((f32[256,128]{1,0:T(8,128)}), f32[2048,128]{1,0:T(8,128)}) %all-gather.4.cloned.1.call-update) | async-done | bytes 1048592 | tf_op jit(solution)/shard_map/all_gather | solution.py:25
  53.1 1.6 multiply_reduce_fusion
  54.7 11.5 %fusion = (f32[1024]{0:T(1024)S(1)}, f32[1024,2048]{1,0:T(8,128)}) fusion(f32[2048]{0:T(1024)S(1)} %bitcast.9, f32[1024,128]{1,0:T(8,128)} %param.3, f32[2048,128]{1,0:T(8,128)} %all-gather.4.cloned.1.call-done, f32[2048]{0:T(1024)S(1)} %multiply_reduce_fusion, f32[1024]{0:T(1024)S(1)} %multiply_reduce_fusion.1), kind=kOutput, calls=%fused_computation.9 | convolution fusion | flops 3233807360 | bytes 9986048 | tf_op jit(solution)/shard_map/dot_general | solution.py:11
  66.2 5.6 %pmax.28 = f32[1024]{0:T(1024)S(1)} all-reduce(f32[1024]{0:T(1024)S(1)} %get-tuple-element.2), channel_id=1, replica_groups=mesh['blk'=8,'tgt'=4] {'tgt'}, use_global_device_ids=true, to_apply=%region_3.0 | all-reduce | flops 1024 | bytes 8192 | tf_op jit(solution)/shard_map/pmax | solution.py:33
  71.8 4.5 %exponential_reduce_fusion.3 = f32[1024]{0:T(1024)S(1)} fusion(f32[1024,2048]{1,0:T(8,128)} %get-tuple-element.3, f32[1024]{0:T(1024)S(1)} %get-tuple-element.2, f32[2048]{0:T(1024)S(1)} %bitcast.10), kind=kLoop, calls=%fused_computation.6 | loop fusion | flops 8387584 | bytes 8404992 | tf_op jit(solution)/shard_map/reduce_sum | solution.py:32
  76.4 6.6 %psum.14 = f32[1024]{0:T(1024)S(1)} all-reduce(f32[1024]{0:T(1024)S(1)} %exponential_multiply_fusion.1), channel_id=1, replica_groups=mesh['blk'=8,'tgt'=4] {'tgt'}, use_global_device_ids=true, to_apply=%region_5.0 | all-reduce | flops 1024 | bytes 8192 | tf_op jit(solution)/shard_map/psum | solution.py:34
  83.0 4.3 %fusion.1 = f32[2048]{0:T(1024)S(1)} fusion(f32[1024,2048]{1,0:T(8,128)} %get-tuple-element.3, f32[1024]{0:T(1024)S(1)} %multiply_subtract_fusion.2), kind=kLoop, calls=%fused_computation.10 | loop fusion | flops 6289408 | bytes 8400896 | tf_op jit(solution)/shard_map/reduce_max | solution.py:38
  87.3 19.4 %pmax.29 = f32[2048]{0:T(1024)S(1)} all-reduce(f32[2048]{0:T(1024)S(1)} %fusion.1), channel_id=1, replica_groups=mesh['blk'=8,'tgt'=4] {'blk'}, use_global_device_ids=true, to_apply=%region_7.0 | all-reduce | flops 2048 | bytes 16384 | tf_op jit(solution)/shard_map/pmax | solution.py:38
  106.7 4.5 %exponential_reduce_fusion.2 = f32[2048]{0:T(1024)S(1)} fusion(f32[1024,2048]{1,0:T(8,128)} %get-tuple-element.3, f32[2048]{0:T(1024)S(1)} %pmax.29, f32[1024]{0:T(1024)S(1)} %multiply_subtract_fusion.2), kind=kLoop, calls=%fused_computation.4 | loop fusion | flops 8386560 | bytes 8409088 | tf_op jit(solution)/shard_map/reduce_sum | solution.py:39
  111.2 17.4 %all-reduce = f32[2048]{0:T(1024)S(1)} all-reduce(f32[2048]{0:T(1024)S(1)} %exponential_reduce_fusion.2), channel_id=2, replica_groups=mesh['blk'=8,'tgt'=4] {'blk'}, use_global_device_ids=true, to_apply=%region_9.0.clone | all-reduce | flops 2048 | bytes 16384
  128.6 0.1 fusion.9
  128.7 18.2 %all-gather.1 = f32[8,1,256]{2,1,0:T(1,128)S(1)} all-gather(f32[1,1,256]{2,1,0:T(1,128)S(1)} %bitcast.11), channel_id=1, replica_groups=mesh['blk'=8,'tgt'=4] {'blk'}, dimensions={0}, use_global_device_ids=true | all-gather | bytes 9216 | tf_op jit(solution)/shard_map/all_gather | solution.py:29
  147.0 4.3 %fusion.2 = f32[1024]{0:T(1024)S(1)} fusion(f32[1024,2048]{1,0:T(8,128)} %get-tuple-element.3, f32[2048]{0:T(1024)S(1)} %bitcast.7), kind=kLoop, calls=%fused_computation.11 | loop fusion | flops 6290432 | bytes 8400896 | tf_op jit(solution)/shard_map/reduce_max | solution.py:31
  151.3 4.5 %exponential_reduce_fusion.1 = f32[1024]{0:T(1024)S(1)} fusion(f32[1024,2048]{1,0:T(8,128)} %get-tuple-element.3, f32[1024]{0:T(1024)S(1)} %fusion.2, f32[2048]{0:T(1024)S(1)} %bitcast.8), kind=kLoop, calls=%fused_computation.2 | loop fusion | flops 8387584 | bytes 8404992 | tf_op jit(solution)/shard_map/reduce_sum | solution.py:32
  155.8 5.7 %pmax.30 = f32[1024]{0:T(1024)S(1)} all-reduce(f32[1024]{0:T(1024)S(1)} %fusion.2), channel_id=1, replica_groups=mesh['blk'=8,'tgt'=4] {'tgt'}, use_global_device_ids=true, to_apply=%region_11.0 | all-reduce | flops 1024 | bytes 8192 | tf_op jit(solution)/shard_map/pmax | solution.py:33
  161.5 6.3 %psum.15 = f32[1024]{0:T(1024)S(1)} all-reduce(f32[1024]{0:T(1024)S(1)} %exponential_multiply_fusion), channel_id=1, replica_groups=mesh['blk'=8,'tgt'=4] {'tgt'}, use_global_device_ids=true, to_apply=%region_13.0 | all-reduce | flops 1024 | bytes 8192 | tf_op jit(solution)/shard_map/psum | solution.py:34
  167.7 0.0 copy-start
  167.7 4.3 %fusion.3 = f32[2048]{0:T(1024)S(1)} fusion(f32[1024,2048]{1,0:T(8,128)} %get-tuple-element.3, f32[1024]{0:T(1024)S(1)} %multiply_subtract_fusion.1), kind=kLoop, calls=%fused_computation.12 | loop fusion | flops 6289408 | bytes 8400896 | tf_op jit(solution)/shard_map/reduce_max | solution.py:38
  172.0 17.4 %pmax.31 = f32[2048]{0:T(1024)S(1)} all-reduce(f32[2048]{0:T(1024)S(1)} %fusion.3), channel_id=1, replica_groups=mesh['blk'=8,'tgt'=4] {'blk'}, use_global_device_ids=true, to_apply=%region_15.0 | all-reduce | flops 2048 | bytes 16384 | tf_op jit(solution)/shard_map/pmax | solution.py:38
  189.4 4.5 %exponential_reduce_fusion = f32[2048]{0:T(1024)S(1)} fusion(f32[1024,2048]{1,0:T(8,128)} %get-tuple-element.3, f32[2048]{0:T(1024)S(1)} %pmax.31, f32[1024]{0:T(1024)S(1)} %multiply_subtract_fusion.1), kind=kLoop, calls=%fused_computation | loop fusion | flops 8386560 | bytes 8409088 | tf_op jit(solution)/shard_map/reduce_sum | solution.py:39
  193.9 0.0 copy-done
  193.9 19.4 %all-reduce.1 = f32[2048]{0:T(1024)S(1)} all-reduce(f32[2048]{0:T(1024)S(1)} %exponential_reduce_fusion), channel_id=3, replica_groups=mesh['blk'=8,'tgt'=4] {'blk'}, use_global_device_ids=true, to_apply=%region_17.0.clone | all-reduce | flops 2048 | bytes 16384
  213.3 0.7 fusion.6
  (4 shorter events, 0.0 us)
Async XLA Ops:
  7.2 46.0 %all-gather.4.cloned.1.call-start = ((), (), s32[]{:S(2)}) async-start(), calls=%async_computation | async-start | bytes 1179648 | tf_op jit(solution)/shard_map/all_gather | solution.py:25
  167.7 26.2 %copy-start = (f32[1024]{0:T(1024)}, f32[1024]{0:T(1024)S(1)}, u32[]{:S(2)}) copy-start(f32[1024]{0:T(1024)S(1)} %multiply_subtract_fusion.1) | copy-start | bytes 12292
Sparse Core Ops, SparseCore 0:
  10.1 42.9 all-gather.3
where the time goes:
time: 221 us
  blocking collectives  139 us (63%)
  other arithmetic  34.5 us (16%)
  waiting for transfers between devices  20.2 us (9%)
  between operations  14.8 us (7%)
  matrix products  11.5 us (5%)
    all_gather x2, blocking collectives, body(): group_pots = lax.all_gather(target_pots, 'blk', axis=0, tiled=True)  40.8 us
    unnamed x2, blocking collectives  36.8 us
    pmax x2, blocking collectives, body(): col_high = lax.pmax(jnp.max(col_scores, axis=0), 'blk')  36.8 us
    all_gather x1, waiting for transfers between devices, body(): group_rows = lax.all_gather(targets, 'blk', axis=0, tiled=True)  19.5 us
    psum x2, blocking collectives, body(): totals = lax.psum(totals * jnp.exp(maxima - highest), 'tgt')  12.9 us
    dot_general x1, matrix products, cost_of(): jnp.dot(left, right.T, preferred_element_type=jnp.float32, precision=lax....  11.5 us
    pmax x2, blocking collectives, body(): highest = lax.pmax(maxima, 'tgt')  11.3 us
    reduce_sum x2, other arithmetic, body(): totals = jnp.sum(jnp.exp(scores - maxima[:, None]), axis=1)  9.01 us
  transfers between devices with their start and end apart: 1, of which 1 were waited for; matrix products, arithmetic and copies ran while one was open for 1% of the time, Pallas kernels for 0%

commit v1 on v0

--- a/solution.py
+++ b/solution.py
@@ -31,7 +31,7 @@
         maxima = jnp.max(scores, axis=1)
         totals = jnp.sum(jnp.exp(scores - maxima[:, None]), axis=1)
         highest = lax.pmax(maxima, "tgt")
-        totals = lax.psum(totals * jnp.exp(maxima - highest), "tgt")
+        totals = jnp.sum(lax.all_gather(totals * jnp.exp(maxima - highest), "tgt"), axis=0)
         maxima = highest
         source_pots = EPS * -jnp.log(jnp.float32(total_dst)) - EPS * (maxima + jnp.log(totals))
         col_scores = (source_pots[:, None] - cost_tile) / EPS

time: 221 us -> 219 us (level)
  blocking collectives: 139 us -> 136 us
    psum x2 -> x0, blocking collectives: 12.9 us -> none  [body(): totals = lax.psum(totals * jnp.exp(maxima - highest), 'tgt')]
    all_gather x0 -> x2, blocking collectives: none -> 10.6 us  [body(): lax.all_gather(totals * jnp.exp(maxima - highest), 'tgt')]
where the time goes in v1:
time: 219 us
  blocking collectives  136 us (62%)
  other arithmetic  34.5 us (16%)
  waiting for transfers between devices  20.2 us (9%)
  between operations  14.8 us (7%)
  matrix products  11.5 us (5%)
    all_gather x2, blocking collectives, body(): group_pots = lax.all_gather(target_pots, 'blk', axis=0, tiled=True)  40.8 us
    pmax x2, blocking collectives, body(): col_high = lax.pmax(jnp.max(col_scores, axis=0), 'blk')  36.8 us
    unnamed x2, blocking collectives  36.8 us
    all_gather x1, waiting for transfers between devices, body(): group_rows = lax.all_gather(targets, 'blk', axis=0, tiled=True)  19.5 us
    dot_general x1, matrix products, cost_of(): jnp.dot(left, right.T, preferred_element_type=jnp.float32, precision=lax....  11.5 us
    pmax x2, blocking collectives, body(): highest = lax.pmax(maxima, 'tgt')  11.3 us
    all_gather x2, blocking collectives, body(): lax.all_gather(totals * jnp.exp(maxima - highest), 'tgt')  10.6 us
    reduce_sum x2, other arithmetic, body(): col_part = jnp.sum(jnp.exp(col_scores - col_high[None, :]), axis=0)  9.01 us
  transfers between devices with their start and end apart: 1, of which 1 were waited for; matrix products, arithmetic and copies ran while one was open for 1% of the time, Pallas kernels for 0%

profile of v1, /device:TPU:0, one launch (start us, length us, event | category | flops | bytes accessed | tf_op | source)
XLA Modules:
  0.0 218.6 jit_solution(49708795191288008)
XLA Ops:
  7.2 0.0 all-gather.6.cloned.1.call-start
  7.2 0.7 all-gather.6.cloned.1.call-update
  7.9 1.2 dynamic-slice
  9.8 22.5 %all-gather.2 = f32[8,1,256]{2,1,0:T(1,128)S(1)} all-gather(f32[1,1,256]{2,1,0:T(1,128)} %bitcast.12), channel_id=1, replica_groups=mesh['blk'=8,'tgt'=4] {'blk'}, dimensions={0}, use_global_device_ids=true | all-gather | bytes 9216 | tf_op jit(solution)/shard_map/all_gather | solution.py:29
  32.3 1.2 multiply_reduce_fusion.1
  33.6 19.5 %all-gather.6.cloned.1.call-done = f32[2048,128]{1,0:T(8,128)} async-done(((f32[256,128]{1,0:T(8,128)}), f32[2048,128]{1,0:T(8,128)}) %all-gather.6.cloned.1.call-update) | async-done | bytes 1048592 | tf_op jit(solution)/shard_map/all_gather | solution.py:25
  53.1 1.6 multiply_reduce_fusion
  54.7 11.5 %fusion = (f32[1024]{0:T(1024)S(1)}, f32[1024,2048]{1,0:T(8,128)}) fusion(f32[2048]{0:T(1024)S(1)} %bitcast.9, f32[1024,128]{1,0:T(8,128)} %param.3, f32[2048,128]{1,0:T(8,128)} %all-gather.6.cloned.1.call-done, f32[2048]{0:T(1024)S(1)} %multiply_reduce_fusion, f32[1024]{0:T(1024)S(1)} %multiply_reduce_fusion.1), kind=kOutput, calls=%fused_computation.9 | convolution fusion | flops 3233807360 | bytes 9986048 | tf_op jit(solution)/shard_map/dot_general | solution.py:11
  66.2 5.6 %pmax.28 = f32[1024]{0:T(1024)S(1)} all-reduce(f32[1024]{0:T(1024)S(1)} %get-tuple-element.2), channel_id=1, replica_groups=mesh['blk'=8,'tgt'=4] {'tgt'}, use_global_device_ids=true, to_apply=%region_3.0 | all-reduce | flops 1024 | bytes 8192 | tf_op jit(solution)/shard_map/pmax | solution.py:33
  71.8 4.5 %exponential_reduce_fusion.3 = f32[1024]{0:T(1024)S(1)} fusion(f32[1024,2048]{1,0:T(8,128)} %get-tuple-element.3, f32[1024]{0:T(1024)S(1)} %get-tuple-element.2, f32[2048]{0:T(1024)S(1)} %bitcast.10), kind=kLoop, calls=%fused_computation.6 | loop fusion | flops 8387584 | bytes 8404992 | tf_op jit(solution)/shard_map/reduce_sum | solution.py:32
  76.4 5.2 %all-gather = f32[4096]{0:T(1024)S(1)} all-gather(f32[1024]{0:T(1024)S(1)} %exponential_multiply_fusion.1), channel_id=2, replica_groups=mesh['blk'=8,'tgt'=4] {'tgt'}, dimensions={0}, use_global_device_ids=true | all-gather | bytes 20480 | tf_op jit(solution)/shard_map/all_gather | solution.py:34
  81.6 4.3 %fusion.1 = f32[2048]{0:T(1024)S(1)} fusion(f32[1024,2048]{1,0:T(8,128)} %get-tuple-element.3, f32[1024]{0:T(1024)S(1)} %multiply_subtract_fusion.2), kind=kLoop, calls=%fused_computation.10 | loop fusion | flops 6289408 | bytes 8400896 | tf_op jit(solution)/shard_map/reduce_max | solution.py:38
  85.9 19.4 %pmax.29 = f32[2048]{0:T(1024)S(1)} all-reduce(f32[2048]{0:T(1024)S(1)} %fusion.1), channel_id=1, replica_groups=mesh['blk'=8,'tgt'=4] {'blk'}, use_global_device_ids=true, to_apply=%region_7.0 | all-reduce | flops 2048 | bytes 16384 | tf_op jit(solution)/shard_map/pmax | solution.py:38
  105.3 4.5 %exponential_reduce_fusion.2 = f32[2048]{0:T(1024)S(1)} fusion(f32[1024,2048]{1,0:T(8,128)} %get-tuple-element.3, f32[2048]{0:T(1024)S(1)} %pmax.29, f32[1024]{0:T(1024)S(1)} %multiply_subtract_fusion.2), kind=kLoop, calls=%fused_computation.4 | loop fusion | flops 8386560 | bytes 8409088 | tf_op jit(solution)/shard_map/reduce_sum | solution.py:39
  109.8 17.4 %all-reduce = f32[2048]{0:T(1024)S(1)} all-reduce(f32[2048]{0:T(1024)S(1)} %exponential_reduce_fusion.2), channel_id=4, replica_groups=mesh['blk'=8,'tgt'=4] {'blk'}, use_global_device_ids=true, to_apply=%region_9.0.clone | all-reduce | flops 2048 | bytes 16384
  127.2 0.1 fusion.9
  127.3 18.3 %all-gather.3 = f32[8,1,256]{2,1,0:T(1,128)S(1)} all-gather(f32[1,1,256]{2,1,0:T(1,128)S(1)} %bitcast.11), channel_id=1, replica_groups=mesh['blk'=8,'tgt'=4] {'blk'}, dimensions={0}, use_global_device_ids=true | all-gather | bytes 9216 | tf_op jit(solution)/shard_map/all_gather | solution.py:29
  145.6 4.3 %fusion.2 = f32[1024]{0:T(1024)S(1)} fusion(f32[1024,2048]{1,0:T(8,128)} %get-tuple-element.3, f32[2048]{0:T(1024)S(1)} %bitcast.7), kind=kLoop, calls=%fused_computation.11 | loop fusion | flops 6290432 | bytes 8400896 | tf_op jit(solution)/shard_map/reduce_max | solution.py:31
  149.9 4.5 %exponential_reduce_fusion.1 = f32[1024]{0:T(1024)S(1)} fusion(f32[1024,2048]{1,0:T(8,128)} %get-tuple-element.3, f32[1024]{0:T(1024)S(1)} %fusion.2, f32[2048]{0:T(1024)S(1)} %bitcast.8), kind=kLoop, calls=%fused_computation.2 | loop fusion | flops 8387584 | bytes 8404992 | tf_op jit(solution)/shard_map/reduce_sum | solution.py:32
  154.4 5.7 %pmax.30 = f32[1024]{0:T(1024)S(1)} all-reduce(f32[1024]{0:T(1024)S(1)} %fusion.2), channel_id=1, replica_groups=mesh['blk'=8,'tgt'=4] {'tgt'}, use_global_device_ids=true, to_apply=%region_11.0 | all-reduce | flops 1024 | bytes 8192 | tf_op jit(solution)/shard_map/pmax | solution.py:33
  160.1 5.4 %all-gather.1 = f32[4096]{0:T(1024)S(1)} all-gather(f32[1024]{0:T(1024)S(1)} %exponential_multiply_fusion), channel_id=3, replica_groups=mesh['blk'=8,'tgt'=4] {'tgt'}, dimensions={0}, use_global_device_ids=true | all-gather | bytes 20480 | tf_op jit(solution)/shard_map/all_gather | solution.py:34
  165.5 0.0 copy-start
  165.5 4.3 %fusion.3 = f32[2048]{0:T(1024)S(1)} fusion(f32[1024,2048]{1,0:T(8,128)} %get-tuple-element.3, f32[1024]{0:T(1024)S(1)} %multiply_subtract_fusion.1), kind=kLoop, calls=%fused_computation.12 | loop fusion | flops 6289408 | bytes 8400896 | tf_op jit(solution)/shard_map/reduce_max | solution.py:38
  169.8 17.4 %pmax.31 = f32[2048]{0:T(1024)S(1)} all-reduce(f32[2048]{0:T(1024)S(1)} %fusion.3), channel_id=1, replica_groups=mesh['blk'=8,'tgt'=4] {'blk'}, use_global_device_ids=true, to_apply=%region_15.0 | all-reduce | flops 2048 | bytes 16384 | tf_op jit(solution)/shard_map/pmax | solution.py:38
  187.2 4.5 %exponential_reduce_fusion = f32[2048]{0:T(1024)S(1)} fusion(f32[1024,2048]{1,0:T(8,128)} %get-tuple-element.3, f32[2048]{0:T(1024)S(1)} %pmax.31, f32[1024]{0:T(1024)S(1)} %multiply_subtract_fusion.1), kind=kLoop, calls=%fused_computation | loop fusion | flops 8386560 | bytes 8409088 | tf_op jit(solution)/shard_map/reduce_sum | solution.py:39
  191.7 0.0 copy-done
  191.7 19.4 %all-reduce.1 = f32[2048]{0:T(1024)S(1)} all-reduce(f32[2048]{0:T(1024)S(1)} %exponential_reduce_fusion), channel_id=5, replica_groups=mesh['blk'=8,'tgt'=4] {'blk'}, use_global_device_ids=true, to_apply=%region_17.0.clone | all-reduce | flops 2048 | bytes 16384
  211.1 0.7 fusion.6
  (8 shorter events, 0.1 us)
Async XLA Ops:
  7.2 46.0 %all-gather.6.cloned.1.call-start = ((), (), s32[]{:S(2)}) async-start(), calls=%async_computation | async-start | bytes 1179648 | tf_op jit(solution)/shard_map/all_gather | solution.py:25
  165.5 26.2 %copy-start = (f32[1024]{0:T(1024)}, f32[1024]{0:T(1024)S(1)}, u32[]{:S(2)}) copy-start(f32[1024]{0:T(1024)S(1)} %multiply_subtract_fusion.1) | copy-start | bytes 12292
Sparse Core Ops, SparseCore 0:
  10.1 42.9 all-gather.5
